TPU v7x, 128 devices: a 2x2x16 block of a 8x8x16 slice. The times are simulated.
128 devices in a mesh: groups: 4 (over x, y), blk: 32 (over z, core).
Axes of the slice: x: 2, y: 2, z: 16, core: 2. Of those that a mesh axis runs over, the one named last changes fastest.
The devices are a block of a 8x8x16 slice.
Arguments:
- coords: float32 [32, 98304], P(None, ('groups', 'blk')), parts along dimension 1, may hold values from -6 to 6
- alpha: float32 [98304], P(('groups', 'blk')), parts along dimension 0, may hold values from -6 to 6
- probe_solves: float32 [15, 98304], P(None, ('groups', 'blk')), parts along dimension 1, may hold values from -6 to 6
- probes: float32 [15, 98304], P(None, ('groups', 'blk')), parts along dimension 1, may hold values from -6 to 6
- lengthscale: float32 [32], replicated, may hold values from 4 to 12
Outputs:
- grad: float32 [32, 98304], P(None, ('groups', 'blk')), parts along dimension 1
There are 4 independent parts, one for each index of `groups`. A program takes and returns all parts, laid end to end along the dimension named above; an argument that names none is the same for every part. Nothing has to cross between parts.
All inputs are finite; a program needn't handle non-finite values.
Results may differ from a plain program's by a relative error of at most 0.00014.
Values sent between devices are 32-bit elements; how exact they have to be, the bound alone decides.
No kernel may reach another device: no remote copies, remote signals or barrier semaphores. Data moves between devices by JAX's collectives and lax.ppermute only.
A program may use at most 64 MiB of HBM per device.

v0:
```python
import jax
import jax.numpy as jnp
from jax import lax
from jax.sharding import PartitionSpec as P

root_five = 5.0**0.5


def shifted(value, axis, steps):
    count = lax.axis_size(axis)
    pairs = [(source, (source + steps) % count) for source in range(count)]
    return lax.ppermute(value, axis, pairs)


def tile_terms(own_scaled, own_table, vis_scaled, vis_table):
    probe_count = (own_table.shape[0] - 1) // 2
    half_inv = 1.0 / (2.0 * probe_count)
    left_rows = jnp.concatenate([own_table[:1], -half_inv * own_table[1:]], 0)
    right_rows = jnp.concatenate(
        [vis_table[:1], vis_table[1 + probe_count :], vis_table[1 : 1 + probe_count]], 0
    )
    contract_first = (((0,), (0,)), ((), ()))
    inner = lax.dot_general(
        own_scaled,
        vis_scaled,
        contract_first,
        precision=lax.Precision.HIGHEST,
        preferred_element_type=jnp.float32,
    )
    own_square = jnp.sum(own_scaled * own_scaled, 0)
    vis_square = jnp.sum(vis_scaled * vis_scaled, 0)
    distance = own_square[:, None] + vis_square[None, :] - 2.0 * inner
    radius = jnp.sqrt(jnp.maximum(distance, 0.0))
    profile = (1.0 + root_five * radius) * jnp.exp(-root_five * radius)
    coupling = lax.dot_general(
        left_rows,
        right_rows,
        contract_first,
        precision=lax.Precision.HIGHEST,
        preferred_element_type=jnp.float32,
    )
    weighted = coupling * profile
    row_part = own_scaled * jnp.sum(weighted, 1)[None, :] - lax.dot_general(
        vis_scaled,
        weighted,
        (((1,), (1,)), ((), ())),
        precision=lax.Precision.HIGHEST,
        preferred_element_type=jnp.float32,
    )
    col_part = vis_scaled * jnp.sum(weighted, 0)[None, :] - jnp.dot(
        own_scaled, weighted, precision=lax.Precision.HIGHEST, preferred_element_type=jnp.float32
    )
    return (row_part, col_part)


def on_device(coords, alpha, probe_solves, probes, lengthscale):
    scaled = coords / lengthscale[:, None]
    table = jnp.concatenate([alpha[None], probe_solves, probes], 0)
    step_count = lax.axis_size("blk") // 4
    vis_scaled, vis_table = shifted((scaled, table), "blk", -1)
    zero_field = jnp.zeros(scaled.shape, jnp.float32)

    def carry_step(index, state):
        cur_scaled, cur_table, col_acc, row_total = state
        row_part, col_part = tile_terms(scaled, table, cur_scaled, cur_table)
        moved = shifted((cur_scaled, cur_table, col_acc + col_part), "blk", -1)
        return (moved[0], moved[1], moved[2], row_total + row_part)

    cur_scaled, cur_table, col_acc, row_total = lax.fori_loop(
        0, step_count - 1, carry_step, (vis_scaled, vis_table, zero_field, zero_field)
    )
    row_part, col_part = tile_terms(scaled, table, cur_scaled, cur_table)
    row_total = row_total + row_part
    col_total = shifted(col_acc + col_part, "blk", step_count)
    return -(5.0 / 3.0) / lengthscale[:, None] * (row_total + col_total)


def solution(mesh):
    return jax.shard_map(
        on_device,
        mesh=mesh,
        in_specs=(
            P(None, ("groups", "blk")),
            P(("groups", "blk")),
            P(None, ("groups", "blk")),
            P(None, ("groups", "blk")),
            P(),
        ),
        out_specs=P(None, ("groups", "blk")),
        check_vma=False,
    )
```

profile of v0, /device:TPU:69, one launch (start us, length us, event | category | flops | bytes accessed | tf_op | source)
XLA Modules:
  0.0 128.9 jit_solution(11084534594902752604)
XLA Ops:
  1.0 9.9 %collective-permute-start.3 = (f32[32,768]{1,0:T(8,128)S(1)}, f32[32,768]{1,0:T(8,128)S(1)}, u32[]{:S(2)}, u32[]{:S(2)}) collective-permute-start(f32[32,768]{1,0:T(8,128)S(1)} %get-tuple-element.244), channel_id=1, source_target_pairs={{0,31},{1,0},{2,1},{3,2},{4,3},{5,4},{6,5},{7,6},{8,7},{9,8},{10,9... | collective-permute-start | bytes 294920 | tf_op jit(solution)/shard_map/ppermute | solution.py:12
  12.5 3.6 %collective-permute-start.4 = (f32[31,768]{1,0:T(8,128)S(1)}, f32[31,768]{1,0:T(8,128)S(1)}, u32[]{:S(2)}, u32[]{:S(2)}) collective-permute-start(f32[31,768]{1,0:T(8,128)S(1)} %fusion.14), channel_id=1, source_target_pairs={{0,31},{1,0},{2,1},{3,2},{4,3},{5,4},{6,5},{7,6},{8,7},{9,8},{10,9... | collective-permute-start | bytes 285704 | tf_op jit(solution)/shard_map/ppermute | solution.py:12
  17.6 92.7 %while.19 = (s32[]{:T(128)}, f32[32,768]{1,0:T(8,128)S(1)}, f32[31,768]{1,0:T(8,128)S(1)}, f32[32,768]{1,0:T(8,128)S(1)}, f32[32,768]{1,0:T(8,128)S(1)}, /*index...) while((s32[]{:T(128)}, f32[32,768]{1,0:T(8,128)S(1)}, ...), condition=%wide.region_5.0_spmd.clone, body=%wide.region_1.5_spmd.clone.sunk | while | flops 905693184 | bytes 15019247 | solution.py:69
  19.0 3.1 %collective-permute-start.1 = (f32[31,768]{1,0:T(8,128)S(1)}, f32[31,768]{1,0:T(8,128)S(1)}, u32[]{:S(2)}, u32[]{:S(2)}) collective-permute-start(f32[31,768]{1,0:T(8,128)S(1)} %copy.13), channel_id=1, source_target_pairs={{0,31},{1,0},{2,1},{3,2},{4,3},{5,4},{6,5},{7,6},{8,7},{9,8},{10,9... | collective-permute-start | bytes 285704 | tf_op jit(solution)/shard_map/while/body/eval_jaxpr/ppermute | solution.py:12
  22.1 2.1 %fusion.62 = f32[768,768]{1,0:T(8,128)S(1)} fusion(f32[30,768]{1,0:T(8,128)S(1)} %slice_multiply_fusion.2, f32[1,768]{1,0:T(1,128)S(1)} %get-tuple-element.264, f32[15,768]{1,0:T(8,128)S(1)} %get-tuple-element.231, f32[15,768]{1,0:T(8,128)S(1)} %get-tuple-element.232, f32[1,768]{1,0:T(1,128)S(1)} %slice.50), kind=kOutput, calls=%fused_computation.7.clone.1 | convolution fusion | flops 219485952 | bytes 2549760 | tf_op jit(solution)/shard_map/while/body/eval_jaxpr/dot_general | solution.py:35
  24.2 3.5 %fusion.63 = (f32[768]{0:T(1024)S(1)}, f32[768]{0:T(1024)S(1)}, f32[768,768]{1,0:T(8,128)S(1)}) fusion(f32[768,768]{1,0:T(8,128)S(1)} %fusion.62, f32[32,768]{1,0:T(8,128)S(1)} %get-tuple-element.266, f32[32,768]{1,0:T(8,128)S(1)} %copy.12, f32[768]{0:T(1024)S(1)} %multiply_reduce_fusion.4, f32[768]{0:T(1024)S(1)} %get-tuple-element.265), kind=kOutput, calls=%fused_computation.39.clone.1 | convolution fusion | flops 232978944 | bytes 4927488 | tf_op jit(solution)/shard_map/while/body/eval_jaxpr/dot_general | solution.py:23
  29.4 2.2 %fusion.65 = f32[32,768]{1,0:T(8,128)S(1)} fusion(f32[768,768]{1,0:T(8,128)S(1)} %get-tuple-element.233, f32[32,768]{1,0:T(8,128)S(1)} %copy.12, f32[32,768]{1,0:T(8,128)S(1)} %get-tuple-element.251, f32[32,768]{1,0:T(8,128)S(1)} %get-tuple-element.266, f32[768]{0:T(1024)S(1)} %get-tuple-element.235, pred[]{:T(512)S(6)} %compare.3), kind=kOutput, calls=%fused_computation.6.clone.1 | convolution fusion | flops 226590720 | bytes 2755585 | tf_op jit(solution)/shard_map/while/body/eval_jaxpr/dot_general | solution.py:43
  36.9 3.5 %fusion.63 = (f32[768]{0:T(1024)S(1)}, f32[768]{0:T(1024)S(1)}, f32[768,768]{1,0:T(8,128)S(1)}) fusion(f32[768,768]{1,0:T(8,128)S(1)} %fusion.62, f32[32,768]{1,0:T(8,128)S(1)} %get-tuple-element.266, f32[32,768]{1,0:T(8,128)S(1)} %copy.12, f32[768]{0:T(1024)S(1)} %multiply_reduce_fusion.4, f32[768]{0:T(1024)S(1)} %get-tuple-element.265), kind=kOutput, calls=%fused_computation.39.clone.1 | convolution fusion | flops 232978944 | bytes 4927488 | tf_op jit(solution)/shard_map/while/body/eval_jaxpr/dot_general | solution.py:23
  42.0 2.2 %fusion.65 = f32[32,768]{1,0:T(8,128)S(1)} fusion(f32[768,768]{1,0:T(8,128)S(1)} %get-tuple-element.233, f32[32,768]{1,0:T(8,128)S(1)} %copy.12, f32[32,768]{1,0:T(8,128)S(1)} %get-tuple-element.251, f32[32,768]{1,0:T(8,128)S(1)} %get-tuple-element.266, f32[768]{0:T(1024)S(1)} %get-tuple-element.235, pred[]{:T(512)S(6)} %compare.3), kind=kOutput, calls=%fused_computation.6.clone.1 | convolution fusion | flops 226590720 | bytes 2755585 | tf_op jit(solution)/shard_map/while/body/eval_jaxpr/dot_general | solution.py:43
  49.6 3.5 %fusion.63 = (f32[768]{0:T(1024)S(1)}, f32[768]{0:T(1024)S(1)}, f32[768,768]{1,0:T(8,128)S(1)}) fusion(f32[768,768]{1,0:T(8,128)S(1)} %fusion.62, f32[32,768]{1,0:T(8,128)S(1)} %get-tuple-element.266, f32[32,768]{1,0:T(8,128)S(1)} %copy.12, f32[768]{0:T(1024)S(1)} %multiply_reduce_fusion.4, f32[768]{0:T(1024)S(1)} %get-tuple-element.265), kind=kOutput, calls=%fused_computation.39.clone.1 | convolution fusion | flops 232978944 | bytes 4927488 | tf_op jit(solution)/shard_map/while/body/eval_jaxpr/dot_general | solution.py:23
  54.7 2.2 %fusion.65 = f32[32,768]{1,0:T(8,128)S(1)} fusion(f32[768,768]{1,0:T(8,128)S(1)} %get-tuple-element.233, f32[32,768]{1,0:T(8,128)S(1)} %copy.12, f32[32,768]{1,0:T(8,128)S(1)} %get-tuple-element.251, f32[32,768]{1,0:T(8,128)S(1)} %get-tuple-element.266, f32[768]{0:T(1024)S(1)} %get-tuple-element.235, pred[]{:T(512)S(6)} %compare.3), kind=kOutput, calls=%fused_computation.6.clone.1 | convolution fusion | flops 226590720 | bytes 2755585 | tf_op jit(solution)/shard_map/while/body/eval_jaxpr/dot_general | solution.py:43
  62.2 3.5 %fusion.63 = (f32[768]{0:T(1024)S(1)}, f32[768]{0:T(1024)S(1)}, f32[768,768]{1,0:T(8,128)S(1)}) fusion(f32[768,768]{1,0:T(8,128)S(1)} %fusion.62, f32[32,768]{1,0:T(8,128)S(1)} %get-tuple-element.266, f32[32,768]{1,0:T(8,128)S(1)} %copy.12, f32[768]{0:T(1024)S(1)} %multiply_reduce_fusion.4, f32[768]{0:T(1024)S(1)} %get-tuple-element.265), kind=kOutput, calls=%fused_computation.39.clone.1 | convolution fusion | flops 232978944 | bytes 4927488 | tf_op jit(solution)/shard_map/while/body/eval_jaxpr/dot_general | solution.py:23
  67.4 2.2 %fusion.65 = f32[32,768]{1,0:T(8,128)S(1)} fusion(f32[768,768]{1,0:T(8,128)S(1)} %get-tuple-element.233, f32[32,768]{1,0:T(8,128)S(1)} %copy.12, f32[32,768]{1,0:T(8,128)S(1)} %get-tuple-element.251, f32[32,768]{1,0:T(8,128)S(1)} %get-tuple-element.266, f32[768]{0:T(1024)S(1)} %get-tuple-element.235, pred[]{:T(512)S(6)} %compare.3), kind=kOutput, calls=%fused_computation.6.clone.1 | convolution fusion | flops 226590720 | bytes 2755585 | tf_op jit(solution)/shard_map/while/body/eval_jaxpr/dot_general | solution.py:43
  71.5 2.2 %collective-permute-start.1 = (f32[31,768]{1,0:T(8,128)S(1)}, f32[31,768]{1,0:T(8,128)S(1)}, u32[]{:S(2)}, u32[]{:S(2)}) collective-permute-start(f32[31,768]{1,0:T(8,128)S(1)} %copy.13), channel_id=1, source_target_pairs={{0,31},{1,0},{2,1},{3,2},{4,3},{5,4},{6,5},{7,6},{8,7},{9,8},{10,9... | collective-permute-start | bytes 285704 | tf_op jit(solution)/shard_map/while/body/eval_jaxpr/ppermute | solution.py:12
  75.9 3.5 %fusion.63 = (f32[768]{0:T(1024)S(1)}, f32[768]{0:T(1024)S(1)}, f32[768,768]{1,0:T(8,128)S(1)}) fusion(f32[768,768]{1,0:T(8,128)S(1)} %fusion.62, f32[32,768]{1,0:T(8,128)S(1)} %get-tuple-element.266, f32[32,768]{1,0:T(8,128)S(1)} %copy.12, f32[768]{0:T(1024)S(1)} %multiply_reduce_fusion.4, f32[768]{0:T(1024)S(1)} %get-tuple-element.265), kind=kOutput, calls=%fused_computation.39.clone.1 | convolution fusion | flops 232978944 | bytes 4927488 | tf_op jit(solution)/shard_map/while/body/eval_jaxpr/dot_general | solution.py:23
  81.0 2.2 %fusion.65 = f32[32,768]{1,0:T(8,128)S(1)} fusion(f32[768,768]{1,0:T(8,128)S(1)} %get-tuple-element.233, f32[32,768]{1,0:T(8,128)S(1)} %copy.12, f32[32,768]{1,0:T(8,128)S(1)} %get-tuple-element.251, f32[32,768]{1,0:T(8,128)S(1)} %get-tuple-element.266, f32[768]{0:T(1024)S(1)} %get-tuple-element.235, pred[]{:T(512)S(6)} %compare.3), kind=kOutput, calls=%fused_computation.6.clone.1 | convolution fusion | flops 226590720 | bytes 2755585 | tf_op jit(solution)/shard_map/while/body/eval_jaxpr/dot_general | solution.py:43
  88.6 3.5 %fusion.63 = (f32[768]{0:T(1024)S(1)}, f32[768]{0:T(1024)S(1)}, f32[768,768]{1,0:T(8,128)S(1)}) fusion(f32[768,768]{1,0:T(8,128)S(1)} %fusion.62, f32[32,768]{1,0:T(8,128)S(1)} %get-tuple-element.266, f32[32,768]{1,0:T(8,128)S(1)} %copy.12, f32[768]{0:T(1024)S(1)} %multiply_reduce_fusion.4, f32[768]{0:T(1024)S(1)} %get-tuple-element.265), kind=kOutput, calls=%fused_computation.39.clone.1 | convolution fusion | flops 232978944 | bytes 4927488 | tf_op jit(solution)/shard_map/while/body/eval_jaxpr/dot_general | solution.py:23
  93.7 2.2 %fusion.65 = f32[32,768]{1,0:T(8,128)S(1)} fusion(f32[768,768]{1,0:T(8,128)S(1)} %get-tuple-element.233, f32[32,768]{1,0:T(8,128)S(1)} %copy.12, f32[32,768]{1,0:T(8,128)S(1)} %get-tuple-element.251, f32[32,768]{1,0:T(8,128)S(1)} %get-tuple-element.266, f32[768]{0:T(1024)S(1)} %get-tuple-element.235, pred[]{:T(512)S(6)} %compare.3), kind=kOutput, calls=%fused_computation.6.clone.1 | convolution fusion | flops 226590720 | bytes 2755585 | tf_op jit(solution)/shard_map/while/body/eval_jaxpr/dot_general | solution.py:43
  101.2 3.5 %fusion.63 = (f32[768]{0:T(1024)S(1)}, f32[768]{0:T(1024)S(1)}, f32[768,768]{1,0:T(8,128)S(1)}) fusion(f32[768,768]{1,0:T(8,128)S(1)} %fusion.62, f32[32,768]{1,0:T(8,128)S(1)} %get-tuple-element.266, f32[32,768]{1,0:T(8,128)S(1)} %copy.12, f32[768]{0:T(1024)S(1)} %multiply_reduce_fusion.4, f32[768]{0:T(1024)S(1)} %get-tuple-element.265), kind=kOutput, calls=%fused_computation.39.clone.1 | convolution fusion | flops 232978944 | bytes 4927488 | tf_op jit(solution)/shard_map/while/body/eval_jaxpr/dot_general | solution.py:23
  106.4 2.2 %fusion.65 = f32[32,768]{1,0:T(8,128)S(1)} fusion(f32[768,768]{1,0:T(8,128)S(1)} %get-tuple-element.233, f32[32,768]{1,0:T(8,128)S(1)} %copy.12, f32[32,768]{1,0:T(8,128)S(1)} %get-tuple-element.251, f32[32,768]{1,0:T(8,128)S(1)} %get-tuple-element.266, f32[768]{0:T(1024)S(1)} %get-tuple-element.235, pred[]{:T(512)S(6)} %compare.3), kind=kOutput, calls=%fused_computation.6.clone.1 | convolution fusion | flops 226590720 | bytes 2755585 | tf_op jit(solution)/shard_map/while/body/eval_jaxpr/dot_general | solution.py:43
  112.5 3.5 %fusion.24 = (f32[768]{0:T(1024)S(1)}, f32[768]{0:T(1024)S(1)}, f32[768,768]{1,0:T(8,128)S(1)}) fusion(f32[768,768]{1,0:T(8,128)S(1)} %fusion.15, f32[32,768]{1,0:T(8,128)S(1)} %get-tuple-element.271, f32[32,768]{1,0:T(8,128)S(1)} %get-tuple-element.109, f32[768]{0:T(1024)S(1)} %multiply_reduce_fusion.1, f32[768]{0:T(1024)S(1)} %get-tuple-element.283), kind=kOutput, calls=%fused_computation.40 | convolution fusion | flops 232978944 | bytes 4927488 | tf_op jit(solution)/shard_map/dot_general | solution.py:23
  117.5 3.0 %collective-permute-start.5 = (f32[32,768]{1,0:T(8,128)S(1)}, f32[32,768]{1,0:T(8,128)S(1)}, u32[]{:S(2)}, u32[]{:S(2)}) collective-permute-start(f32[32,768]{1,0:T(8,128)S(1)} %subtract_add_fusion), channel_id=1, source_target_pairs={{0,8},{1,9},{2,10},{3,11},{4,12},{5,13},{6,14},{7,15},{8,16},{9,17... | collective-permute-start | bytes 294920 | tf_op jit(solution)/shard_map/ppermute | solution.py:12
  120.5 2.2 %convolution_subtract_fusion = f32[32,768]{1,0:T(8,128)S(1)} fusion(f32[32,768]{1,0:T(8,128)S(1)} %get-tuple-element.109, f32[768,768]{1,0:T(8,128)S(1)} %get-tuple-element.170, f32[32,768]{1,0:T(8,128)S(1)} %get-tuple-element.271, f32[768]{0:T(1024)S(1)} %get-tuple-element.143), kind=kOutput, calls=%fused_computation.20 | convolution fusion | flops 226541568 | bytes 2657280 | tf_op jit(solution)/shard_map/dot_general | solution.py:43
  122.7 5.4 %collective-permute-done.5 = f32[32,768]{1,0:T(8,128)S(1)} collective-permute-done((f32[32,768]{1,0:T(8,128)S(1)}, f32[32,768]{1,0:T(8,128)S(1)}, u32[]{:S(2)}, u32[]{:S(2)}) %collective-permute-start.5) | collective-permute-done | bytes 98336 | tf_op jit(solution)/shard_map/ppermute | solution.py:12
  (111 shorter events, 53.0 us)
Async XLA Ops:
  1.0 16.6 %collective-permute-start.3 = (f32[32,768]{1,0:T(8,128)S(1)}, f32[32,768]{1,0:T(8,128)S(1)}, u32[]{:S(2)}, u32[]{:S(2)}) collective-permute-start(f32[32,768]{1,0:T(8,128)S(1)} %get-tuple-element.244), channel_id=1, source_target_pairs={{0,31},{1,0},{2,1},{3,2},{4,3},{5,4},{6,5},{7,6},{8,7},{9,8},{10,9... | collective-permute-start | bytes 294920 | tf_op jit(solution)/shard_map/ppermute | solution.py:12
  12.5 5.1 %collective-permute-start.4 = (f32[31,768]{1,0:T(8,128)S(1)}, f32[31,768]{1,0:T(8,128)S(1)}, u32[]{:S(2)}, u32[]{:S(2)}) collective-permute-start(f32[31,768]{1,0:T(8,128)S(1)} %fusion.14), channel_id=1, source_target_pairs={{0,31},{1,0},{2,1},{3,2},{4,3},{5,4},{6,5},{7,6},{8,7},{9,8},{10,9... | collective-permute-start | bytes 285704 | tf_op jit(solution)/shard_map/ppermute | solution.py:12
  17.6 15.7 %collective-permute-start = (f32[32,768]{1,0:T(8,128)S(1)}, f32[32,768]{1,0:T(8,128)S(1)}, u32[]{:S(2)}, u32[]{:S(2)}) collective-permute-start(f32[32,768]{1,0:T(8,128)S(1)} %copy.12), channel_id=1, source_target_pairs={{0,31},{1,0},{2,1},{3,2},{4,3},{5,4},{6,5},{7,6},{8,7},{9,8},{10,9... | collective-permute-start | bytes 294920 | tf_op jit(solution)/shard_map/while/body/eval_jaxpr/ppermute | solution.py:12
  19.0 12.6 %collective-permute-start.1 = (f32[31,768]{1,0:T(8,128)S(1)}, f32[31,768]{1,0:T(8,128)S(1)}, u32[]{:S(2)}, u32[]{:S(2)}) collective-permute-start(f32[31,768]{1,0:T(8,128)S(1)} %copy.13), channel_id=1, source_target_pairs={{0,31},{1,0},{2,1},{3,2},{4,3},{5,4},{6,5},{7,6},{8,7},{9,8},{10,9... | collective-permute-start | bytes 285704 | tf_op jit(solution)/shard_map/while/body/eval_jaxpr/ppermute | solution.py:12
  29.3 4.1 %collective-permute-start.2 = (f32[32,768]{1,0:T(8,128)S(1)}, f32[32,768]{1,0:T(8,128)S(1)}, u32[]{:S(2)}, u32[]{:S(2)}) collective-permute-start(f32[32,768]{1,0:T(8,128)S(1)} %fusion.64), channel_id=1, source_target_pairs={{0,31},{1,0},{2,1},{3,2},{4,3},{5,4},{6,5},{7,6},{8,7},{9,8},{10,9... | collective-permute-start | bytes 294920 | tf_op jit(solution)/shard_map/while/body/eval_jaxpr/ppermute | solution.py:12
  33.4 12.7 %collective-permute-start = (f32[32,768]{1,0:T(8,128)S(1)}, f32[32,768]{1,0:T(8,128)S(1)}, u32[]{:S(2)}, u32[]{:S(2)}) collective-permute-start(f32[32,768]{1,0:T(8,128)S(1)} %copy.12), channel_id=1, source_target_pairs={{0,31},{1,0},{2,1},{3,2},{4,3},{5,4},{6,5},{7,6},{8,7},{9,8},{10,9... | collective-permute-start | bytes 294920 | tf_op jit(solution)/shard_map/while/body/eval_jaxpr/ppermute | solution.py:12
  33.5 10.8 %collective-permute-start.1 = (f32[31,768]{1,0:T(8,128)S(1)}, f32[31,768]{1,0:T(8,128)S(1)}, u32[]{:S(2)}, u32[]{:S(2)}) collective-permute-start(f32[31,768]{1,0:T(8,128)S(1)} %copy.13), channel_id=1, source_target_pairs={{0,31},{1,0},{2,1},{3,2},{4,3},{5,4},{6,5},{7,6},{8,7},{9,8},{10,9... | collective-permute-start | bytes 285704 | tf_op jit(solution)/shard_map/while/body/eval_jaxpr/ppermute | solution.py:12
  41.9 4.1 %collective-permute-start.2 = (f32[32,768]{1,0:T(8,128)S(1)}, f32[32,768]{1,0:T(8,128)S(1)}, u32[]{:S(2)}, u32[]{:S(2)}) collective-permute-start(f32[32,768]{1,0:T(8,128)S(1)} %fusion.64), channel_id=1, source_target_pairs={{0,31},{1,0},{2,1},{3,2},{4,3},{5,4},{6,5},{7,6},{8,7},{9,8},{10,9... | collective-permute-start | bytes 294920 | tf_op jit(solution)/shard_map/while/body/eval_jaxpr/ppermute | solution.py:12
  46.0 12.7 %collective-permute-start = (f32[32,768]{1,0:T(8,128)S(1)}, f32[32,768]{1,0:T(8,128)S(1)}, u32[]{:S(2)}, u32[]{:S(2)}) collective-permute-start(f32[32,768]{1,0:T(8,128)S(1)} %copy.12), channel_id=1, source_target_pairs={{0,31},{1,0},{2,1},{3,2},{4,3},{5,4},{6,5},{7,6},{8,7},{9,8},{10,9... | collective-permute-start | bytes 294920 | tf_op jit(solution)/shard_map/while/body/eval_jaxpr/ppermute | solution.py:12
  46.1 10.8 %collective-permute-start.1 = (f32[31,768]{1,0:T(8,128)S(1)}, f32[31,768]{1,0:T(8,128)S(1)}, u32[]{:S(2)}, u32[]{:S(2)}) collective-permute-start(f32[31,768]{1,0:T(8,128)S(1)} %copy.13), channel_id=1, source_target_pairs={{0,31},{1,0},{2,1},{3,2},{4,3},{5,4},{6,5},{7,6},{8,7},{9,8},{10,9... | collective-permute-start | bytes 285704 | tf_op jit(solution)/shard_map/while/body/eval_jaxpr/ppermute | solution.py:12
  54.6 4.1 %collective-permute-start.2 = (f32[32,768]{1,0:T(8,128)S(1)}, f32[32,768]{1,0:T(8,128)S(1)}, u32[]{:S(2)}, u32[]{:S(2)}) collective-permute-start(f32[32,768]{1,0:T(8,128)S(1)} %fusion.64), channel_id=1, source_target_pairs={{0,31},{1,0},{2,1},{3,2},{4,3},{5,4},{6,5},{7,6},{8,7},{9,8},{10,9... | collective-permute-start | bytes 294920 | tf_op jit(solution)/shard_map/while/body/eval_jaxpr/ppermute | solution.py:12
  58.7 12.7 %collective-permute-start = (f32[32,768]{1,0:T(8,128)S(1)}, f32[32,768]{1,0:T(8,128)S(1)}, u32[]{:S(2)}, u32[]{:S(2)}) collective-permute-start(f32[32,768]{1,0:T(8,128)S(1)} %copy.12), channel_id=1, source_target_pairs={{0,31},{1,0},{2,1},{3,2},{4,3},{5,4},{6,5},{7,6},{8,7},{9,8},{10,9... | collective-permute-start | bytes 294920 | tf_op jit(solution)/shard_map/while/body/eval_jaxpr/ppermute | solution.py:12
  58.8 10.8 %collective-permute-start.1 = (f32[31,768]{1,0:T(8,128)S(1)}, f32[31,768]{1,0:T(8,128)S(1)}, u32[]{:S(2)}, u32[]{:S(2)}) collective-permute-start(f32[31,768]{1,0:T(8,128)S(1)} %copy.13), channel_id=1, source_target_pairs={{0,31},{1,0},{2,1},{3,2},{4,3},{5,4},{6,5},{7,6},{8,7},{9,8},{10,9... | collective-permute-start | bytes 285704 | tf_op jit(solution)/shard_map/while/body/eval_jaxpr/ppermute | solution.py:12
  67.3 4.1 %collective-permute-start.2 = (f32[32,768]{1,0:T(8,128)S(1)}, f32[32,768]{1,0:T(8,128)S(1)}, u32[]{:S(2)}, u32[]{:S(2)}) collective-permute-start(f32[32,768]{1,0:T(8,128)S(1)} %fusion.64), channel_id=1, source_target_pairs={{0,31},{1,0},{2,1},{3,2},{4,3},{5,4},{6,5},{7,6},{8,7},{9,8},{10,9... | collective-permute-start | bytes 294920 | tf_op jit(solution)/shard_map/while/body/eval_jaxpr/ppermute | solution.py:12
  71.4 13.6 %collective-permute-start = (f32[32,768]{1,0:T(8,128)S(1)}, f32[32,768]{1,0:T(8,128)S(1)}, u32[]{:S(2)}, u32[]{:S(2)}) collective-permute-start(f32[32,768]{1,0:T(8,128)S(1)} %copy.12), channel_id=1, source_target_pairs={{0,31},{1,0},{2,1},{3,2},{4,3},{5,4},{6,5},{7,6},{8,7},{9,8},{10,9... | collective-permute-start | bytes 294920 | tf_op jit(solution)/shard_map/while/body/eval_jaxpr/ppermute | solution.py:12
  71.5 11.8 %collective-permute-start.1 = (f32[31,768]{1,0:T(8,128)S(1)}, f32[31,768]{1,0:T(8,128)S(1)}, u32[]{:S(2)}, u32[]{:S(2)}) collective-permute-start(f32[31,768]{1,0:T(8,128)S(1)} %copy.13), channel_id=1, source_target_pairs={{0,31},{1,0},{2,1},{3,2},{4,3},{5,4},{6,5},{7,6},{8,7},{9,8},{10,9... | collective-permute-start | bytes 285704 | tf_op jit(solution)/shard_map/while/body/eval_jaxpr/ppermute | solution.py:12
  80.9 4.1 %collective-permute-start.2 = (f32[32,768]{1,0:T(8,128)S(1)}, f32[32,768]{1,0:T(8,128)S(1)}, u32[]{:S(2)}, u32[]{:S(2)}) collective-permute-start(f32[32,768]{1,0:T(8,128)S(1)} %fusion.64), channel_id=1, source_target_pairs={{0,31},{1,0},{2,1},{3,2},{4,3},{5,4},{6,5},{7,6},{8,7},{9,8},{10,9... | collective-permute-start | bytes 294920 | tf_op jit(solution)/shard_map/while/body/eval_jaxpr/ppermute | solution.py:12
  85.0 12.7 %collective-permute-start = (f32[32,768]{1,0:T(8,128)S(1)}, f32[32,768]{1,0:T(8,128)S(1)}, u32[]{:S(2)}, u32[]{:S(2)}) collective-permute-start(f32[32,768]{1,0:T(8,128)S(1)} %copy.12), channel_id=1, source_target_pairs={{0,31},{1,0},{2,1},{3,2},{4,3},{5,4},{6,5},{7,6},{8,7},{9,8},{10,9... | collective-permute-start | bytes 294920 | tf_op jit(solution)/shard_map/while/body/eval_jaxpr/ppermute | solution.py:12
  85.1 10.8 %collective-permute-start.1 = (f32[31,768]{1,0:T(8,128)S(1)}, f32[31,768]{1,0:T(8,128)S(1)}, u32[]{:S(2)}, u32[]{:S(2)}) collective-permute-start(f32[31,768]{1,0:T(8,128)S(1)} %copy.13), channel_id=1, source_target_pairs={{0,31},{1,0},{2,1},{3,2},{4,3},{5,4},{6,5},{7,6},{8,7},{9,8},{10,9... | collective-permute-start | bytes 285704 | tf_op jit(solution)/shard_map/while/body/eval_jaxpr/ppermute | solution.py:12
  93.6 4.1 %collective-permute-start.2 = (f32[32,768]{1,0:T(8,128)S(1)}, f32[32,768]{1,0:T(8,128)S(1)}, u32[]{:S(2)}, u32[]{:S(2)}) collective-permute-start(f32[32,768]{1,0:T(8,128)S(1)} %fusion.64), channel_id=1, source_target_pairs={{0,31},{1,0},{2,1},{3,2},{4,3},{5,4},{6,5},{7,6},{8,7},{9,8},{10,9... | collective-permute-start | bytes 294920 | tf_op jit(solution)/shard_map/while/body/eval_jaxpr/ppermute | solution.py:12
  97.7 12.7 %collective-permute-start = (f32[32,768]{1,0:T(8,128)S(1)}, f32[32,768]{1,0:T(8,128)S(1)}, u32[]{:S(2)}, u32[]{:S(2)}) collective-permute-start(f32[32,768]{1,0:T(8,128)S(1)} %copy.12), channel_id=1, source_target_pairs={{0,31},{1,0},{2,1},{3,2},{4,3},{5,4},{6,5},{7,6},{8,7},{9,8},{10,9... | collective-permute-start | bytes 294920 | tf_op jit(solution)/shard_map/while/body/eval_jaxpr/ppermute | solution.py:12
  97.8 10.8 %collective-permute-start.1 = (f32[31,768]{1,0:T(8,128)S(1)}, f32[31,768]{1,0:T(8,128)S(1)}, u32[]{:S(2)}, u32[]{:S(2)}) collective-permute-start(f32[31,768]{1,0:T(8,128)S(1)} %copy.13), channel_id=1, source_target_pairs={{0,31},{1,0},{2,1},{3,2},{4,3},{5,4},{6,5},{7,6},{8,7},{9,8},{10,9... | collective-permute-start | bytes 285704 | tf_op jit(solution)/shard_map/while/body/eval_jaxpr/ppermute | solution.py:12
  106.3 4.1 %collective-permute-start.2 = (f32[32,768]{1,0:T(8,128)S(1)}, f32[32,768]{1,0:T(8,128)S(1)}, u32[]{:S(2)}, u32[]{:S(2)}) collective-permute-start(f32[32,768]{1,0:T(8,128)S(1)} %fusion.64), channel_id=1, source_target_pairs={{0,31},{1,0},{2,1},{3,2},{4,3},{5,4},{6,5},{7,6},{8,7},{9,8},{10,9... | collective-permute-start | bytes 294920 | tf_op jit(solution)/shard_map/while/body/eval_jaxpr/ppermute | solution.py:12
  117.5 10.7 %collective-permute-start.5 = (f32[32,768]{1,0:T(8,128)S(1)}, f32[32,768]{1,0:T(8,128)S(1)}, u32[]{:S(2)}, u32[]{:S(2)}) collective-permute-start(f32[32,768]{1,0:T(8,128)S(1)} %subtract_add_fusion), channel_id=1, source_target_pairs={{0,8},{1,9},{2,10},{3,11},{4,12},{5,13},{6,14},{7,15},{8,16},{9,17... | collective-permute-start | bytes 294920 | tf_op jit(solution)/shard_map/ppermute | solution.py:12
where the time goes:
time: 130 us; the launch traced here: 129 us
  matrix products  74.4 us (57%)
  starting transfers between devices  30.7 us (24%)
  waiting for transfers between devices  17.8 us (14%)
  other arithmetic  4.33 us (3%)
    ppermute x24, starting transfers between devices, shifted(): return lax.ppermute(value, axis, pairs)  30.7 us
    dot_general x8, matrix products, tile_terms(): lax.dot_general(own_scaled, vis_scaled, contract_first, precision=lax.Pre...  28.1 us
    ppermute x24, waiting for transfers between devices, shifted(): return lax.ppermute(value, axis, pairs)  17.8 us
    dot_general x8, matrix products, tile_terms(): lax.dot_general(vis_scaled, weighted, (((1,), (1,)), ((), ())), precision...  17.7 us
    dot_general x8, matrix products, tile_terms(): lax.dot_general(left_rows, right_rows, contract_first, precision=lax.Prec...  16.4 us
    dot_general x8, matrix products, tile_terms(): jnp.dot(own_scaled, weighted, precision=lax.Precision.HIGHEST, preferred_...  12.2 us
  transfers between devices with their start and end apart: 24, of which 8 were waited for; matrix products, arithmetic and copies ran while one was open for 55% of the time, Pallas kernels for 0%

commit v1 on v0

v1 whole, which is shorter than its diff:
```python
import functools

import jax
import jax.numpy as jnp
from jax import lax
from jax.experimental import pallas as pl
from jax.experimental.pallas import tpu as pltpu
from jax.sharding import PartitionSpec as P

root_five = 5.0**0.5
minus_log2e = -1.4426950408889634
f32, bf16 = jnp.float32, jnp.bfloat16
VMEM = pl.BlockSpec(memory_space=pltpu.VMEM)
DIM, GROUP, SUMS = 32, 16, 80
STEP = 256


def halves(value):
    high = value.astype(bf16)
    return high, (value - high.astype(f32)).astype(bf16)


def row_is(row, value, other):
    return jnp.where(lax.broadcasted_iota(jnp.int32, other.shape, 0) == row, value, other)


def edge_rows(square, parts_at, ones_at):
    one = square.astype(bf16).astype(f32)
    rest = square - one
    two = rest.astype(bf16).astype(f32)
    row = lax.broadcasted_iota(jnp.int32, square.shape, 0)
    edge = jnp.where((row >= ones_at) & (row < ones_at + 3), 1.0, 0.0)
    for index, part in enumerate((one, two, rest - two)):
        edge = row_is(parts_at + index, part, edge)
    return edge.astype(bf16)


def own_forms(field, dist_ref, coup_ref):
    high, low = halves(field[:DIM])
    first, second = field[DIM : DIM + GROUP], field[DIM + GROUP :]
    square = jnp.broadcast_to(second[:1], first.shape)
    dist_ref[...] = jnp.concatenate([high, low, high, low, edge_rows(square, 3, 0)], 0)
    table = jnp.concatenate([row_is(0, first, second), row_is(0, 0.0, first)], 0)
    high, low = halves(table)
    coup_ref[...] = jnp.concatenate([high, low, high, low], 0)


def visit_forms(half_inv, field, dist_ref, coup_ref, sums_ref):
    points = field.shape[1]
    high, low = halves(field[:DIM])
    first, second = field[DIM : DIM + GROUP], field[DIM + GROUP :]
    sums_ref[...] = jnp.concatenate([high, low, jnp.ones((GROUP, points), bf16)], 0)
    square = jnp.broadcast_to(second[:1], first.shape)
    twice = [-2.0 * high, -2.0 * low]
    zero = jnp.zeros((256 - 4 * DIM - GROUP, points), bf16)
    dist = jnp.concatenate([*twice, *twice[::-1], edge_rows(square, 0, 3), zero], 0)
    dist_ref[...] = dist.T
    table = jnp.concatenate(
        [row_is(0, first, -half_inv * first), row_is(0, 0.0, -half_inv * second)], 0
    )
    high, low = halves(table)
    coup_ref[...] = jnp.concatenate([high, high, low, low], 0).T


def weights(dist, coup):
    dist = jnp.maximum(dist, 1e-30)
    scaled = dist * lax.rsqrt(dist)
    return coup * ((1.0 + scaled) * jnp.exp2(scaled * minus_log2e))


def dot(left, right):
    return lax.dot_general(
        left, right, (((1,), (0,)), ((), ())), preferred_element_type=f32
    )


def add_tile(vis, own, acc_ref, high_ref, low_ref, slot):
    vis_dist, vis_coup, vis_sums = vis
    own_dist, own_coup = own
    points = acc_ref.shape[1]
    depth = own_dist.shape[0]
    width = high_ref.shape[2]
    for start in range(0, points, width):
        cols = slice(start, start + width)
        for begin in range(0, points, STEP):
            rows = slice(begin, begin + STEP)
            dist = dot(vis_dist[rows, :depth], own_dist[:, cols])
            coup = dot(vis_coup[rows, :], own_coup[:, cols])
            high, low = halves(weights(dist, coup))
            high_ref[slot, rows, :] = high
            low_ref[slot, rows, :] = low
        sums = vis_sums[...]
        acc_ref[:, cols] += dot(sums, high_ref[slot]) + dot(sums, low_ref[slot])
        slot = 1 - slot
    return slot


def finish(field, acc):
    high, low = halves(field[:DIM])
    near = high.astype(f32) + low.astype(f32)
    return near * acc[2 * DIM : 2 * DIM + 1] - (acc[:DIM] + acc[DIM : 2 * DIM])


def visit_kernel(half_inv, pairs, n_vis, n_own, n_acc, n_form, done, *refs):
    refs = list(refs)

    def take(count):
        taken, refs[:] = refs[:count], refs[count:]
        return taken

    vis = take(n_vis)
    own = [take(2) for _ in range(n_own)]
    acc_in = take(n_acc)
    fields = take(len(done))
    acc_out = take(n_own)
    forms = [take(2) for _ in range(n_form)]
    outs = take(len(done))
    high_ref, low_ref = take(2)
    for index in range(n_own):
        if index < n_acc:
            acc_out[index][...] = acc_in[index][...]
        else:
            acc_out[index][...] = jnp.zeros_like(acc_out[index])
    for index in range(n_form):
        own_forms(vis[index][...], *forms[index])
    sides = []
    for ref in vis:
        side = take(3)
        visit_forms(half_inv, ref[...], *side)
        sides.append(side)
    slot = 0
    for v, o in pairs:
        slot = add_tile(sides[v], own[o], acc_out[o], high_ref, low_ref, slot)
    for o, field, out in zip(done, fields, outs):
        out[...] = finish(field[...], acc_out[o][...])


def visit(half_inv, pairs, vis, own, accs, n_form=0, done=(), fields=()):
    points = vis[0].shape[1]
    n_own = len(own)
    acc_shape = jax.ShapeDtypeStruct((SUMS, points), f32)
    form_shapes = [
        jax.ShapeDtypeStruct((4 * DIM + GROUP, points), bf16),
        jax.ShapeDtypeStruct((8 * GROUP, points), bf16),
    ]
    out_shape = [acc_shape] * n_own + form_shapes * n_form
    out_shape += [jax.ShapeDtypeStruct((DIM, points), f32)] * len(done)
    scratch = [pltpu.VMEM((2, points, 256), bf16)] * 2
    for _ in vis:
        scratch += [
            pltpu.VMEM((points, 256), bf16),
            pltpu.VMEM((points, 8 * GROUP), bf16),
            pltpu.VMEM((SUMS, points), bf16),
        ]
    args = [*vis, *[ref for forms in own for ref in forms], *accs, *fields]
    first = len(vis) + 2 * n_own
    return pl.pallas_call(
        functools.partial(
            visit_kernel, half_inv, pairs, len(vis), n_own, len(accs), n_form, done
        ),
        out_shape=out_shape,
        in_specs=[VMEM] * len(args),
        out_specs=[VMEM] * len(out_shape),
        scratch_shapes=scratch,
        input_output_aliases={first + index: index for index in range(len(accs))},
        compiler_params=pltpu.CompilerParams(vmem_limit_bytes=20 * 2**20),
        cost_estimate=pl.CostEstimate(
            flops=len(pairs) * 10**9, bytes_accessed=10**6, transcendentals=0
        ),
        name="visit",
    )(*args)


def field_kernel(coords, alpha, solves, probes, length, field, dist_ref, coup_ref):
    size = length.shape[1]
    spread = jnp.broadcast_to(length[...], (size, size))
    row = lax.broadcasted_iota(jnp.int32, (size, size), 0)
    col = lax.broadcasted_iota(jnp.int32, (size, size), 1)
    column = jnp.sum(jnp.where(row == col, spread, 0.0), 1, keepdims=True)
    scaled = coords[...] * (root_five / column)
    high, low = halves(scaled)
    near = high.astype(f32) + low.astype(f32)
    middle = DIM + GROUP
    field[0:DIM, :] = scaled
    field[DIM : DIM + 1, :] = alpha[...]
    field[DIM + 1 : middle, :] = solves[...]
    field[middle : middle + 1, :] = jnp.sum(near * near, 0, keepdims=True)
    field[middle + 1 :, :] = probes[...]
    own_forms(field[...], dist_ref, coup_ref)


def make_field(coords, alpha, solves, probes, lengthscale):
    points = coords.shape[1]
    return pl.pallas_call(
        field_kernel,
        out_shape=[
            jax.ShapeDtypeStruct((DIM + 2 * GROUP, points), f32),
            jax.ShapeDtypeStruct((4 * DIM + GROUP, points), bf16),
            jax.ShapeDtypeStruct((8 * GROUP, points), bf16),
        ],
        in_specs=[VMEM] * 5,
        out_specs=[VMEM] * 3,
        compiler_params=pltpu.CompilerParams(vmem_limit_bytes=8 * 2**20),
        name="field",
    )(coords, alpha[None], solves, probes, lengthscale[None])


def swapped(value):
    count = lax.axis_size("blk")
    return lax.ppermute(value, "blk", [(b, b + 1 - 2 * (b % 2)) for b in range(count)])


def toward(value, even, odd):
    count = lax.axis_size("blk")
    pairs = [(b, (b + (odd if b % 2 else even)) % count) for b in range(count)]
    return lax.ppermute(value, "blk", pairs)


def on_device(coords, alpha, probe_solves, probes, lengthscale):
    half_inv = 1.0 / (2.0 * probes.shape[0])
    hops = lax.axis_size("blk") // 8
    field, *own = make_field(coords, alpha, probe_solves, probes, lengthscale)
    near = toward(field, -2, 2)
    mate = swapped(field)
    cross = toward(field, 3, -3)
    acc, *own_mate = visit(half_inv, ((0, 0),), [mate], [own], [], n_form=1)
    accs = [acc]
    for hop in range(1, hops):
        here, there = near, cross
        near, cross = toward(here, -2, 2), toward(there, -2, 2)
        accs = visit(half_inv, ((0, 0), (0, 1)), [here], [own, own_mate], accs)
        accs = visit(half_inv, ((0, 0), (0, 1)), [there], [own, own_mate], accs)
    _, mine = visit(
        half_inv, ((0, 0),), [near], [own], accs[:1], done=(0,), fields=[field]
    )
    _, theirs = visit(
        half_inv, ((0, 0), (1, 0)), [near, cross], [own_mate], accs[1:], done=(0,), fields=[mate]
    )
    total = mine + swapped(theirs)
    return (-(root_five / 3.0) / lengthscale)[:, None] * total


def solution(mesh):
    return jax.shard_map(
        on_device,
        mesh=mesh,
        in_specs=(
            P(None, ("groups", "blk")),
            P(("groups", "blk")),
            P(None, ("groups", "blk")),
            P(None, ("groups", "blk")),
            P(),
        ),
        out_specs=P(None, ("groups", "blk")),
        check_vma=False,
    )
```

time: 130 us -> 57.5 us (0.44)
  matrix products: 74.4 us -> 0 us
  Pallas kernels: 0 us -> 24.6 us
  waiting for transfers between devices: 17.8 us -> 6.21 us
  starting transfers between devices: 30.7 us -> 21.7 us
  other arithmetic: 4.33 us -> 0.72 us
  local copies, waits for them, and re-layouts: 0.9 us -> 3.83 us
    dot_general x32 -> x0, matrix products: 74.4 us -> none  [the longest x8 28.1 us: tile_terms(): lax.dot_general(own_scaled, vis_scaled, contract_first, precision=lax.Pre...]
    pallas_call x0 -> x10, Pallas kernels: none -> 24.6 us  [the longest x9 24.5 us: visit(): pl.pallas_call(functools.partial(visit_kernel, half_inv, pairs, len(vis),...]
    ppermute x24 -> x10, waiting for transfers between devices: 17.8 us -> 6.21 us  [the longest x8 6.21 us: toward(): return lax.ppermute(value, 'blk', pairs)]
    ppermute x24 -> x10, starting transfers between devices: 30.7 us -> 21.7 us  [the longest x8 15 us: toward(): return lax.ppermute(value, 'blk', pairs)]
    unnamed x0 -> x8, local copies, waits for them, and re-layouts: none -> 3.14 us
  transfers between devices with their start and end apart: 24 -> 10, of which waited for: 8 -> 4; matrix products, arithmetic and copies ran while one was open for 55% -> 0% of each run, Pallas kernels for 0% -> 38%
where the time goes in v1:
time: 57.5 us; the launch traced here: 57.2 us
  Pallas kernels  24.6 us (43%)
  starting transfers between devices  21.7 us (38%)
  waiting for transfers between devices  6.21 us (11%)
  local copies, waits for them, and re-layouts  3.83 us (7%)
  other arithmetic  0.72 us (1%)
    pallas_call x9, Pallas kernels, visit(): pl.pallas_call(functools.partial(visit_kernel, half_inv, pairs, len(vis),...  24.5 us
    ppermute x8, starting transfers between devices, toward(): return lax.ppermute(value, 'blk', pairs)  15 us
    ppermute x2, starting transfers between devices, swapped(): lax.ppermute(value, 'blk', [(b, b + 1 - 2 * (b % 2)) for b in range(count)])  6.69 us
    ppermute x8, waiting for transfers between devices, toward(): return lax.ppermute(value, 'blk', pairs)  6.21 us
    unnamed x8, local copies, waits for them, and re-layouts  3.14 us
  transfers between devices with their start and end apart: 10, of which 4 were waited for; matrix products, arithmetic and copies ran while one was open for 0% of the time, Pallas kernels for 38%

profile of v1, /device:TPU:69, one launch (start us, length us, event | category | flops | bytes accessed | tf_op | source)
XLA Modules:
  0.0 57.2 jit_solution(11096268085822524106)
XLA Ops:
  0.0 0.7 %broadcast_in_dim.7.alpha = f32[1,768]{1,0:T(1,128)S(1)} reshape(f32[768]{0:T(1024)} %param.6) | data formatting | bytes 6144 | tf_op jit(solution)/shard_map/broadcast_in_dim | solution.py:205
  0.7 0.7 %copy-done.3 = f32[32]{0:T(128)S(1)} copy-done((f32[32]{0:T(128)S(1)}, f32[32]{0:T(128)}, u32[]{:S(2)}) %copy-start.3) | copy-done | bytes 152
  1.3 0.9 %copy-done = f32[32,768]{1,0:T(8,128)S(1)} copy-done((f32[32,768]{1,0:T(8,128)S(1)}, f32[32,768]{1,0:T(8,128)}, u32[]{:S(2)}) %copy-start) | copy-done | bytes 98328
  2.2 0.8 %copy-done.1 = f32[15,768]{1,0:T(8,128)S(1)} copy-done((f32[15,768]{1,0:T(8,128)S(1)}, f32[15,768]{1,0:T(8,128)}, u32[]{:S(2)}) %copy-start.1) | copy-done | bytes 46104
  3.0 0.8 %copy-done.2 = f32[15,768]{1,0:T(8,128)S(1)} copy-done((f32[15,768]{1,0:T(8,128)S(1)}, f32[15,768]{1,0:T(8,128)}, u32[]{:S(2)}) %copy-start.2) | copy-done | bytes 46104
  3.8 0.1 field.1
  4.0 2.8 %collective-permute-start = (f32[64,768]{1,0:T(8,128)S(1)}, f32[64,768]{1,0:T(8,128)S(1)}, u32[]{:S(2)}, u32[]{:S(2)}) collective-permute-start(f32[64,768]{1,0:T(8,128)S(1)} %get-tuple-element.25.refs_4_), channel_id=1, source_target_pairs={{0,30},{1,3},{2,0},{3,5},{4,2},{5,7},{6,4},{7,9},{8,6},{9,11},{10,... | collective-permute-start | bytes 589832 | tf_op jit(solution)/shard_map/ppermute | solution.py:216
  6.8 11.7 %collective-permute-start.4 = (f32[64,768]{1,0:T(8,128)S(1)}, f32[64,768]{1,0:T(8,128)S(1)}, u32[]{:S(2)}, u32[]{:S(2)}) collective-permute-start(f32[64,768]{1,0:T(8,128)S(1)} %get-tuple-element.25.refs_4_), channel_id=1, source_target_pairs={{0,3},{1,30},{2,5},{3,0},{4,7},{5,2},{6,9},{7,4},{8,11},{9,6},{10,... | collective-permute-start | bytes 589832 | tf_op jit(solution)/shard_map/ppermute | solution.py:216
  18.5 2.3 %collective-permute-done.refs_0_ = f32[64,768]{1,0:T(8,128)S(1)} collective-permute-done((f32[64,768]{1,0:T(8,128)S(1)}, f32[64,768]{1,0:T(8,128)S(1)}, u32[]{:S(2)}, u32[]{:S(2)}) %collective-permute-start) | collective-permute-done | bytes 196640 | tf_op jit(solution)/shard_map/ppermute | solution.py:216
  20.8 2.2 %collective-permute-done.4.refs_0_ = f32[64,768]{1,0:T(8,128)S(1)} collective-permute-done((f32[64,768]{1,0:T(8,128)S(1)}, f32[64,768]{1,0:T(8,128)S(1)}, u32[]{:S(2)}, u32[]{:S(2)}) %collective-permute-start.4) | collective-permute-done | bytes 196640 | tf_op jit(solution)/shard_map/ppermute | solution.py:216
  23.0 1.6 %visit.9 = (f32[80,768]{1,0:T(8,128)S(1)}, bf16[144,768]{1,0:T(8,128)(2,1)S(1)}, bf16[128,768]{1,0:T(8,128)(2,1)S(1)}) custom-call(f32[64,768]{1,0:T(8,128)S(1)} %collective-permute-done.7.refs_0_.refs_5_, bf16[144,768]{1,0:T(8,128)(2,1)S(1)} %get-tuple-element.26.refs_1_, bf16[128,768]{1,0:T(8,128)(2,1)S(1)} %get-tuple-element.27.refs_2_), custom_call_target="tpu_custom_call" | custom-call | flops 1000000000 | bytes 1000000 | tf_op jit(solution)/shard_map/visit/pallas_call | solution.py:157
  24.6 3.0 %visit.10 = (f32[80,768]{1,0:T(8,128)S(1)}, f32[80,768]{1,0:T(8,128)S(1)}) custom-call(f32[64,768]{1,0:T(8,128)S(1)} %collective-permute-done.refs_0_, bf16[144,768]{1,0:T(8,128)(2,1)S(1)} %get-tuple-element.26.refs_1_, bf16[128,768]{1,0:T(8,128)(2,1)S(1)} %get-tuple-element.27.refs_2_, ...), custom_call_target="tpu_custom_call", output_to_operand_aliasing={{0}: (5, {})} | custom-call | flops 2000000000 | bytes 1000000 | tf_op jit(solution)/shard_map/visit/pallas_call | solution.py:157
  27.6 3.0 %visit.11 = (f32[80,768]{1,0:T(8,128)S(1)}, f32[80,768]{1,0:T(8,128)S(1)}) custom-call(f32[64,768]{1,0:T(8,128)S(1)} %collective-permute-done.4.refs_0_, bf16[144,768]{1,0:T(8,128)(2,1)S(1)} %get-tuple-element.26.refs_1_, bf16[128,768]{1,0:T(8,128)(2,1)S(1)} %get-tuple-element.27.refs_2_, ...), custom_call_target="tpu_custom_call", output_to_operand_aliasing={{0}: (5, {}), {1}: (6, {})} | custom-call | flops 2000000000 | bytes 1000000 | tf_op jit(solution)/shard_map/visit/pallas_call | solution.py:157
  30.8 0.3 collective-permute-start.6
  31.2 3.0 %visit.12 = (f32[80,768]{1,0:T(8,128)S(1)}, f32[80,768]{1,0:T(8,128)S(1)}) custom-call(f32[64,768]{1,0:T(8,128)S(1)} %collective-permute-done.1.refs_0_, bf16[144,768]{1,0:T(8,128)(2,1)S(1)} %get-tuple-element.26.refs_1_, bf16[128,768]{1,0:T(8,128)(2,1)S(1)} %get-tuple-element.27.refs_2_, ...), custom_call_target="tpu_custom_call", output_to_operand_aliasing={{0}: (5, {}), {1}: (6, {})} | custom-call | flops 2000000000 | bytes 1000000 | tf_op jit(solution)/shard_map/visit/pallas_call | solution.py:157
  34.2 3.0 %visit.13 = (f32[80,768]{1,0:T(8,128)S(1)}, f32[80,768]{1,0:T(8,128)S(1)}) custom-call(f32[64,768]{1,0:T(8,128)S(1)} %collective-permute-done.5.refs_0_, bf16[144,768]{1,0:T(8,128)(2,1)S(1)} %get-tuple-element.26.refs_1_, bf16[128,768]{1,0:T(8,128)(2,1)S(1)} %get-tuple-element.27.refs_2_, ...), custom_call_target="tpu_custom_call", output_to_operand_aliasing={{0}: (5, {}), {1}: (6, {})} | custom-call | flops 2000000000 | bytes 1000000 | tf_op jit(solution)/shard_map/visit/pallas_call | solution.py:157
  37.4 1.3 %collective-permute-done.6.refs_0_ = f32[64,768]{1,0:T(8,128)S(1)} collective-permute-done((f32[64,768]{1,0:T(8,128)S(1)}, f32[64,768]{1,0:T(8,128)S(1)}, u32[]{:S(2)}, u32[]{:S(2)}) %collective-permute-start.6) | collective-permute-done | bytes 196640 | tf_op jit(solution)/shard_map/ppermute | solution.py:216
  38.7 3.0 %visit.14 = (f32[80,768]{1,0:T(8,128)S(1)}, f32[80,768]{1,0:T(8,128)S(1)}) custom-call(f32[64,768]{1,0:T(8,128)S(1)} %collective-permute-done.2.refs_0_, bf16[144,768]{1,0:T(8,128)(2,1)S(1)} %get-tuple-element.26.refs_1_, bf16[128,768]{1,0:T(8,128)(2,1)S(1)} %get-tuple-element.27.refs_2_, ...), custom_call_target="tpu_custom_call", output_to_operand_aliasing={{0}: (5, {}), {1}: (6, {})} | custom-call | flops 2000000000 | bytes 1000000 | tf_op jit(solution)/shard_map/visit/pallas_call | solution.py:157
  41.7 3.0 %visit.15 = (f32[80,768]{1,0:T(8,128)S(1)}, f32[80,768]{1,0:T(8,128)S(1)}) custom-call(f32[64,768]{1,0:T(8,128)S(1)} %collective-permute-done.6.refs_0_, bf16[144,768]{1,0:T(8,128)(2,1)S(1)} %get-tuple-element.26.refs_1_, bf16[128,768]{1,0:T(8,128)(2,1)S(1)} %get-tuple-element.27.refs_2_, ...), custom_call_target="tpu_custom_call", output_to_operand_aliasing={{0}: (5, {}), {1}: (6, {})} | custom-call | flops 2000000000 | bytes 1000000 | tf_op jit(solution)/shard_map/visit/pallas_call | solution.py:157
  44.8 0.4 collective-permute-done.8.refs_1_
  45.2 2.9 %visit.17 = (f32[80,768]{1,0:T(8,128)S(1)}, f32[32,768]{1,0:T(8,128)S(1)}) custom-call(f32[64,768]{1,0:T(8,128)S(1)} %collective-permute-done.3.refs_0_, f32[64,768]{1,0:T(8,128)S(1)} %collective-permute-done.8.refs_1_, bf16[144,768]{1,0:T(8,128)(2,1)S(1)} %get-tuple-element.28.refs_3_.refs_2_, ...), custom_call_target="tpu_custom_call", output_to_operand_aliasing={{0}: (4, {})} | custom-call | flops 2000000000 | bytes 1000000 | tf_op jit(solution)/shard_map/visit/pallas_call | solution.py:157
  48.1 6.7 %collective-permute-start.9 = (f32[32,768]{1,0:T(8,128)S(1)}, f32[32,768]{1,0:T(8,128)S(1)}, u32[]{:S(2)}, u32[]{:S(2)}) collective-permute-start(f32[32,768]{1,0:T(8,128)S(1)} %get-tuple-element.44), channel_id=1, source_target_pairs={{0,1},{1,0},{2,3},{3,2},{4,5},{5,4},{6,7},{7,6},{8,9},{9,8},{10,11... | collective-permute-start | bytes 294920 | tf_op jit(solution)/shard_map/ppermute | solution.py:210
  54.8 1.7 %visit.16 = (f32[80,768]{1,0:T(8,128)S(1)}, f32[32,768]{1,0:T(8,128)S(1)}) custom-call(f32[64,768]{1,0:T(8,128)S(1)} %collective-permute-done.3.refs_0_, bf16[144,768]{1,0:T(8,128)(2,1)S(1)} %get-tuple-element.26.refs_1_, bf16[128,768]{1,0:T(8,128)(2,1)S(1)} %get-tuple-element.27.refs_2_, ...), custom_call_target="tpu_custom_call", output_to_operand_aliasing={{0}: (3, {})} | custom-call | flops 1000000000 | bytes 1000000 | tf_op jit(solution)/shard_map/visit/pallas_call | solution.py:157
  56.5 0.7 %add_multiply_fusion = f32[32,768]{1,0:T(8,128)} fusion(f32[32,768]{1,0:T(8,128)S(1)} %get-tuple-element.42, f32[32,768]{1,0:T(8,128)S(1)} %collective-permute-done.9, f32[32]{0:T(128)S(1)} %broadcast_divide_fusion), kind=kLoop, calls=%fused_computation | loop fusion | flops 49152 | bytes 295040 | tf_op jit(solution)/shard_map/mul | solution.py:240
  (17 shorter events, 0.3 us)
Async XLA Ops:
  0.7 0.7 %copy-start.3 = (f32[32]{0:T(128)S(1)}, f32[32]{0:T(128)}, u32[]{:S(2)}) copy-start(f32[32]{0:T(128)} %param.9) | copy-start | bytes 388
  1.3 0.9 %copy-start = (f32[32,768]{1,0:T(8,128)S(1)}, f32[32,768]{1,0:T(8,128)}, u32[]{:S(2)}) copy-start(f32[32,768]{1,0:T(8,128)} %coords.1) | copy-start | bytes 294916
  2.2 0.8 %copy-start.1 = (f32[15,768]{1,0:T(8,128)S(1)}, f32[15,768]{1,0:T(8,128)}, u32[]{:S(2)}) copy-start(f32[15,768]{1,0:T(8,128)} %solves.1) | copy-start | bytes 138244
  3.0 0.8 %copy-start.2 = (f32[15,768]{1,0:T(8,128)S(1)}, f32[15,768]{1,0:T(8,128)}, u32[]{:S(2)}) copy-start(f32[15,768]{1,0:T(8,128)} %probes.1) | copy-start | bytes 138244
  4.0 16.8 %collective-permute-start = (f32[64,768]{1,0:T(8,128)S(1)}, f32[64,768]{1,0:T(8,128)S(1)}, u32[]{:S(2)}, u32[]{:S(2)}) collective-permute-start(f32[64,768]{1,0:T(8,128)S(1)} %get-tuple-element.25.refs_4_), channel_id=1, source_target_pairs={{0,30},{1,3},{2,0},{3,5},{4,2},{5,7},{6,4},{7,9},{8,6},{9,11},{10,... | collective-permute-start | bytes 589832 | tf_op jit(solution)/shard_map/ppermute | solution.py:216
  6.8 16.2 %collective-permute-start.4 = (f32[64,768]{1,0:T(8,128)S(1)}, f32[64,768]{1,0:T(8,128)S(1)}, u32[]{:S(2)}, u32[]{:S(2)}) collective-permute-start(f32[64,768]{1,0:T(8,128)S(1)} %get-tuple-element.25.refs_4_), channel_id=1, source_target_pairs={{0,3},{1,30},{2,5},{3,0},{4,7},{5,2},{6,9},{7,4},{8,11},{9,6},{10,... | collective-permute-start | bytes 589832 | tf_op jit(solution)/shard_map/ppermute | solution.py:216
  18.5 4.5 %collective-permute-start.7 = (f32[64,768]{1,0:T(8,128)S(1)}, f32[64,768]{1,0:T(8,128)S(1)}, u32[]{:S(2)}, u32[]{:S(2)}) collective-permute-start(f32[64,768]{1,0:T(8,128)S(1)} %get-tuple-element.25.refs_4_), channel_id=1, source_target_pairs={{0,1},{1,0},{2,3},{3,2},{4,5},{5,4},{6,7},{7,6},{8,9},{9,8},{10,11... | collective-permute-start | bytes 589832 | tf_op jit(solution)/shard_map/ppermute | solution.py:210
  20.8 9.9 %collective-permute-start.1 = (f32[64,768]{1,0:T(8,128)S(1)}, f32[64,768]{1,0:T(8,128)S(1)}, u32[]{:S(2)}, u32[]{:S(2)}) collective-permute-start(f32[64,768]{1,0:T(8,128)S(1)} %collective-permute-done.refs_0_), channel_id=1, source_target_pairs={{0,30},{1,3},{2,0},{3,5},{4,2},{5,7},{6,4},{7,9},{8,6},{9,11},{10,... | collective-permute-start | bytes 589832 | tf_op jit(solution)/shard_map/ppermute | solution.py:216
  22.9 7.9 %collective-permute-start.5 = (f32[64,768]{1,0:T(8,128)S(1)}, f32[64,768]{1,0:T(8,128)S(1)}, u32[]{:S(2)}, u32[]{:S(2)}) collective-permute-start(f32[64,768]{1,0:T(8,128)S(1)} %collective-permute-done.4.refs_0_), channel_id=1, source_target_pairs={{0,30},{1,3},{2,0},{3,5},{4,2},{5,7},{6,4},{7,9},{8,6},{9,11},{10,... | collective-permute-start | bytes 589832 | tf_op jit(solution)/shard_map/ppermute | solution.py:216
  30.7 6.6 %collective-permute-start.2 = (f32[64,768]{1,0:T(8,128)S(1)}, f32[64,768]{1,0:T(8,128)S(1)}, u32[]{:S(2)}, u32[]{:S(2)}) collective-permute-start(f32[64,768]{1,0:T(8,128)S(1)} %collective-permute-done.1.refs_0_), channel_id=1, source_target_pairs={{0,30},{1,3},{2,0},{3,5},{4,2},{5,7},{6,4},{7,9},{8,6},{9,11},{10,... | collective-permute-start | bytes 589832 | tf_op jit(solution)/shard_map/ppermute | solution.py:216
  30.8 7.8 %collective-permute-start.6 = (f32[64,768]{1,0:T(8,128)S(1)}, f32[64,768]{1,0:T(8,128)S(1)}, u32[]{:S(2)}, u32[]{:S(2)}) collective-permute-start(f32[64,768]{1,0:T(8,128)S(1)} %collective-permute-done.5.refs_0_), channel_id=1, source_target_pairs={{0,30},{1,3},{2,0},{3,5},{4,2},{5,7},{6,4},{7,9},{8,6},{9,11},{10,... | collective-permute-start | bytes 589832 | tf_op jit(solution)/shard_map/ppermute | solution.py:216
  37.3 7.5 %collective-permute-start.3 = (f32[64,768]{1,0:T(8,128)S(1)}, f32[64,768]{1,0:T(8,128)S(1)}, u32[]{:S(2)}, u32[]{:S(2)}) collective-permute-start(f32[64,768]{1,0:T(8,128)S(1)} %collective-permute-done.2.refs_0_), channel_id=1, source_target_pairs={{0,30},{1,3},{2,0},{3,5},{4,2},{5,7},{6,4},{7,9},{8,6},{9,11},{10,... | collective-permute-start | bytes 589832 | tf_op jit(solution)/shard_map/ppermute | solution.py:216
  38.7 6.6 %collective-permute-start.8 = (f32[64,768]{1,0:T(8,128)S(1)}, f32[64,768]{1,0:T(8,128)S(1)}, u32[]{:S(2)}, u32[]{:S(2)}) collective-permute-start(f32[64,768]{1,0:T(8,128)S(1)} %collective-permute-done.6.refs_0_), channel_id=1, source_target_pairs={{0,30},{1,3},{2,0},{3,5},{4,2},{5,7},{6,4},{7,9},{8,6},{9,11},{10,... | collective-permute-start | bytes 589832 | tf_op jit(solution)/shard_map/ppermute | solution.py:216
  48.1 8.4 %collective-permute-start.9 = (f32[32,768]{1,0:T(8,128)S(1)}, f32[32,768]{1,0:T(8,128)S(1)}, u32[]{:S(2)}, u32[]{:S(2)}) collective-permute-start(f32[32,768]{1,0:T(8,128)S(1)} %get-tuple-element.44), channel_id=1, source_target_pairs={{0,1},{1,0},{2,3},{3,2},{4,5},{5,4},{6,7},{7,6},{8,9},{9,8},{10,11... | collective-permute-start | bytes 294920 | tf_op jit(solution)/shard_map/ppermute | solution.py:210
